TPU v7x, 32 devices: a whole 2x2x4 slice. The times are simulated.
32 devices in a mesh: grp: 8 (over y, x, core), inner: 4 (over z).
Axes of the slice: x: 2, y: 2, z: 4, core: 2. Of those that a mesh axis runs over, the one named last changes fastest.
Arguments:
- amplitudes: bfloat16 [16, 8, 12288], P('grp', None, 'inner'), may hold values from -6 to 6
- factors: bfloat16 [16, 2000, 12288], P('grp', 'inner'), may hold values from -0.125 to 0.125
- atom_charges: bfloat16 [16, 64, 12288], P('grp', None, 'inner'), may hold values from -0.0068359375 to 0.0068359375
- eps_occ: float32 [16, 48], P('grp'), may hold values from -1.2 to -0.3
- eps_vir: float32 [16, 256], P('grp'), may hold values from 0.1 to 1.5
- occ_count: int32 [16], P('grp'), may hold values from 24 to 48
- vir_count: int32 [16], P('grp'), may hold values from 128 to 256
- atom_list: int32 [1024], P('grp'), may hold values from 0 to 1023, each once
- positions: float32 [3, 1024], replicated, may hold values from 0 to 12
Outputs:
- refined: float32 [16, 8, 12288], P('grp', None, 'inner')
- hamiltonian: float32 [128, 8, 16], P('grp', None, 'inner')
Inputs may be any that keep to these rules, and one draw needn't show every extreme that they name: `atom_list`: every atom index appears exactly once.
All inputs are finite; a program needn't handle non-finite values.
Results may differ from a plain program's by a relative error of at most 0.022.
Values may be sent and summed in bfloat16 or wider, within the bound.
No kernel may reach another device: no remote copies, remote signals or barrier semaphores. Data moves between devices by JAX's collectives and lax.ppermute only.
A program may use at most 64 MiB of HBM per device.

v0:
```python
import jax
import jax.numpy as jnp
from jax import lax
from jax.sharding import PartitionSpec as P

NVIR = 256
STATES = 8
epsilon = 1e-06


def coupling_block(
    group_charges, own_xyz, own_ids, energies, in_charges, in_xyz, slice_rows, inner_pos, monomers
):
    count = in_charges.shape[0]
    offset = own_xyz[:, :, :, None, None] - jnp.transpose(in_xyz, (1, 0, 2))[None, :, None, :, :]
    kernel = 1.0 / jnp.sqrt(jnp.sum(offset * offset, axis=1) + 1.0)
    block = jnp.einsum(
        "csa,carb,rb->csr", group_charges, kernel, in_charges, precision=lax.Precision.HIGHEST
    )
    column = jnp.arange(count, dtype=jnp.int32)
    source = column // slice_rows
    within = inner_pos * slice_rows + column % slice_rows
    in_ids = source * monomers + within // STATES
    in_state = within % STATES
    same = own_ids[:, None, None] == in_ids[None, None, :]
    diag = jnp.arange(STATES, dtype=jnp.int32)[None, :, None] == in_state[None, None, :]
    block = jnp.where(same, jnp.where(diag, energies[:, :, None], 0.0), block)
    return block.reshape(monomers * STATES, count)


def local(
    amplitudes, factors, atom_charges, eps_occ, eps_vir, occ_count, vir_count, atom_list, positions
):
    monomers, states_here, local_pairs = amplitudes.shape
    atom_count = atom_charges.shape[1]
    inner_count = lax.axis_size("inner")
    inner_pos = lax.axis_index("inner")
    pair_index = inner_pos * local_pairs + jnp.arange(local_pairs, dtype=jnp.int32)
    occ_of = pair_index // NVIR
    vir_of = pair_index % NVIR
    active = (
        (occ_of[None, :] < occ_count[:, None]) & (vir_of[None, :] < vir_count[:, None])
    ).astype(jnp.float32)
    gap = jnp.take(eps_vir, vir_of, axis=1) - jnp.take(eps_occ, occ_of, axis=1)
    masked = amplitudes * active[:, None, :].astype(jnp.bfloat16)
    fitted = jnp.einsum(
        "cso,cqo->csq",
        lax.all_gather(masked, "inner", axis=2, tiled=True),
        factors,
        preferred_element_type=jnp.float32,
    )
    fitted_low = fitted.astype(jnp.bfloat16)
    current = masked.astype(jnp.float32)
    partial_value = (
        2.0 * jnp.einsum("csq,cqo->cso", fitted_low, factors, preferred_element_type=jnp.float32)
    ).astype(jnp.bfloat16)
    coulomb = lax.psum_scatter(partial_value, "inner", scatter_dimension=2, tiled=True).astype(
        jnp.float32
    )
    image = gap[:, None, :] * current + coulomb * active[:, None, :]
    numerator, squares = lax.psum(
        (jnp.sum(current * image, axis=2), jnp.sum(current * current, axis=2)), "inner"
    )
    energies = numerator / (squares + epsilon)
    refined = active[:, None, :] * (
        current - (image - energies[:, :, None] * current) / gap[:, None, :]
    )
    refined_low = refined.astype(jnp.bfloat16)
    partial_charges = jnp.einsum(
        "cso,cao->csa", refined_low, atom_charges, preferred_element_type=jnp.float32
    ).reshape(monomers * states_here, atom_count)
    slice_rows = monomers * states_here // inner_count
    group_charges = lax.psum(partial_charges, "inner")
    slice_charges = lax.dynamic_slice_in_dim(group_charges, inner_pos * slice_rows, slice_rows, 0)
    group_charges = group_charges.reshape(monomers, states_here, atom_count)
    own_xyz = (
        jnp.take(positions, atom_list, axis=1).reshape(3, monomers, atom_count).transpose(1, 0, 2)
    )
    slice_index = inner_pos * slice_rows + jnp.arange(slice_rows, dtype=jnp.int32)
    slice_xyz = jnp.take(own_xyz, slice_index // STATES, axis=0)
    group_pos = lax.axis_index("grp")
    groups = lax.axis_size("grp")
    own_ids = group_pos * monomers + jnp.arange(monomers, dtype=jnp.int32)
    block = coupling_block(
        group_charges,
        own_xyz,
        own_ids,
        energies,
        lax.all_gather(slice_charges, "grp", axis=0, tiled=True),
        lax.all_gather(slice_xyz, "grp", axis=0, tiled=True),
        slice_rows,
        inner_pos,
        monomers,
    )
    return (refined, block.reshape(monomers * states_here, groups, slice_rows))


def solution(mesh):
    in_specs = (
        P("grp", None, "inner"),
        P("grp", "inner", None),
        P("grp", None, "inner"),
        P("grp", None),
        P("grp", None),
        P("grp"),
        P("grp"),
        P("grp"),
        P(),
    )
    out_specs = (P("grp", None, "inner"), P("grp", None, "inner"))
    return jax.shard_map(local, mesh=mesh, in_specs=in_specs, out_specs=out_specs, check_vma=False)
```

profile of v0, /device:TPU:0, one launch (start us, length us, event | category | flops | bytes accessed | tf_op | source)
XLA Modules:
  0.0 175.4 jit_solution(12270682259931202777)
XLA Ops:
  7.3 0.8 fusion.36
  8.1 0.9 broadcast_multiply_fusion
  9.0 16.3 %all_gather.9 = bf16[2,8,12288]{2,1,0:T(8,128)(2,1)S(1)} all-gather(bf16[2,8,3072]{2,1,0:T(8,128)(2,1)S(1)} %broadcast_multiply_fusion), channel_id=1, replica_groups=mesh['grp'=8,'inner'=4] {'inner'}, dimensions={2}, use_global_device_ids=true | all-gather | bytes 491520 | tf_op jit(solution)/shard_map/all_gather | solution.py:48
  25.3 64.8 %fusion.7 = bf16[2,8,12288]{2,1,0:T(8,128)(2,1)} fusion(bf16[2,500,12288]{2,0,1:T(2,128)(2,1)} %param.10, bf16[2,8,12288]{2,1,0:T(8,128)(2,1)S(1)} %all_gather.9), kind=kOutput, calls=%fused_computation.9 | convolution fusion | flops 393617216 | bytes 25362432 | tf_op jit(solution)/shard_map/csq,cqo->cso/dot_general | solution.py:55
  90.1 0.1 compare_select_fusion
  90.3 0.1 copy.45
  90.5 0.1 copy.46
  90.6 10.8 %gather_fusion = f32[3072,2]{1,0:T(8,128)} fusion(f32[2,256]{0,1:T(8,128)S(1)} %copy.45, s32[3072]{0:T(1024)S(1)} %broadcast_clamp_fusion.1), kind=kCustom, calls=%fused_computation | custom fusion | bytes 61440 | tf_op jit(solution)/shard_map/jit(_take)/gather | solution.py:44
  101.4 10.8 %gather_fusion.1 = f32[3072,2]{1,0:T(8,128)} fusion(f32[2,48]{0,1:T(8,128)S(1)} %copy.46, s32[3072]{0:T(1024)S(1)} %broadcast_clamp_fusion), kind=kCustom, calls=%fused_computation.1 | custom fusion | bytes 61440 | tf_op jit(solution)/shard_map/jit(_take)/gather | solution.py:44
  112.2 3.8 %subtract_bitcast_fusion = f32[2,3072]{0,1:T(8,128)S(1)} fusion(f32[3072,2]{1,0:T(8,128)} %gather_fusion.1, f32[3072,2]{1,0:T(8,128)} %gather_fusion, pred[3072]{0:T(1024)(128)(4,1)S(1)} %get-tuple-element.14, pred[3072]{0:T(1024)(128)(4,1)S(1)} %get-tuple-element.15), kind=kLoop, calls=%fused_computation.14 | loop fusion | flops 18432 | bytes 79872 | tf_op jit(solution)/shard_map/sub | solution.py:44
  116.0 0.5 copy.47
  116.5 0.2 copy.50
  116.7 0.6 gather_fusion.2
  117.4 0.1 copy.51
  117.4 0.1 broadcast_in_dim.94
  117.6 0.6 gather_fusion.3
  118.1 0.1 broadcast_select_fusion
  118.2 9.2 %all_gather.10 = f32[32,3,64]{2,1,0:T(4,128)S(1)} all-gather(f32[4,3,64]{2,1,0:T(4,128)S(1)} %broadcast_select_fusion), channel_id=1, replica_groups=mesh['grp'=8,'inner'=4] {'grp'}, dimensions={0}, use_global_device_ids=true | all-gather | bytes 27648 | tf_op jit(solution)/shard_map/all_gather | solution.py:90
  127.5 0.1 broadcast_compare_fusion
  127.5 1.1 multiply_reduce_fusion
  128.7 0.3 add_rsqrt_fusion
  129.0 0.6 copy-done.1
  129.6 1.1 fusion.19
  130.6 12.4 %all-reduce = (f32[2,8]{1,0:T(2,128)S(1)}, f32[2,8]{1,0:T(2,128)S(1)}) all-reduce(f32[2,8]{1,0:T(2,128)S(1)} %get-tuple-element.5, f32[2,8]{1,0:T(2,128)S(1)} %get-tuple-element.4), channel_id=1, replica_groups=mesh['grp'=8,'inner'=4] {'inner'}, use_global_device_ids=true, to_apply=%region_2.3 | all-reduce | flops 32 | bytes 256 | tf_op jit(solution)/shard_map/psum | solution.py:61
  143.1 1.0 fusion.22
  144.1 0.3 convolution_bitcast_fusion
  144.4 8.5 %psum.23 = f32[16,64]{1,0:T(8,128)S(1)} all-reduce(f32[16,64]{1,0:T(8,128)S(1)} %convolution_bitcast_fusion), channel_id=1, replica_groups=mesh['grp'=8,'inner'=4] {'inner'}, use_global_device_ids=true, to_apply=%region_5.6 | all-reduce | flops 1024 | bytes 8192 | tf_op jit(solution)/shard_map/psum | solution.py:73
  152.9 8.9 %all-gather = f32[8,4,64]{2,1,0:T(4,128)S(1)} all-gather(f32[1,4,64]{2,1,0:T(4,128)S(1)} %dynamic-slice_bitcast_fusion), channel_id=1, replica_groups=mesh['grp'=8,'inner'=4] {'grp'}, dimensions={0}, use_global_device_ids=true | all-gather | bytes 9216 | tf_op jit(solution)/shard_map/all_gather | solution.py:89
  161.8 5.8 %fusion.10 = f32[32,1,2,64]{3,1,2,0:T(1,128)S(1)} fusion(f32[32,64,1,1]{1,2,3,0:T(1,128)S(1)} %bitcast.34, f32[2,64,32,64]{3,2,1,0:T(8,128)S(1)} %add_rsqrt_fusion), kind=kOutput, calls=%fused_computation.11 | convolution fusion | flops 3145728 | bytes 1073152 | tf_op jit(solution)/shard_map/csa,carb,rb->csr/dot_general | solution.py:17
  167.6 0.2 convolution_select_fusion
  167.8 0.1 copy.53
  167.9 0.7 reshape_reshape.3
  (33 shorter events, 0.3 us)
Async XLA Ops:
  7.2 136.9 %copy-start = (bf16[2,64,3072]{2,1,0:T(8,128)(2,1)S(1)}, bf16[2,64,3072]{2,1,0:T(8,128)(2,1)}, u32[]{:S(2)}) copy-start(bf16[2,64,3072]{2,1,0:T(8,128)(2,1)} %param.11) | copy-start | bytes 2359300
  7.2 121.8 %reduce-scatter.2.cloned.1.call-start = ((), (), s32[]{:S(2)}) async-start(), calls=%async_computation.1 | async-start | bytes 491520 | tf_op jit(solution)/shard_map/reduce_scatter | solution.py:57
  25.3 65.0 %copy-start.6 = (s32[128]{0:T(128)S(1)}, s32[128]{0:T(128)}, u32[]{:S(2)}) copy-start(s32[128]{0:T(128)} %param.16) | copy-start | bytes 1540
  25.3 65.1 %copy-start.4 = (f32[2,256]{1,0:T(2,128)S(1)}, f32[2,256]{1,0:T(2,128)}, u32[]{:S(2)}) copy-start(f32[2,256]{1,0:T(2,128)} %param.13) | copy-start | bytes 6148
  25.3 65.2 %copy-start.5 = (f32[2,48]{1,0:T(2,128)S(1)}, f32[2,48]{1,0:T(2,128)}, u32[]{:S(2)}) copy-start(f32[2,48]{1,0:T(2,128)} %param.12) | copy-start | bytes 1156
  112.2 4.3 %copy-start.3 = (f32[3,1024]{1,0:T(4,128)S(1)}, f32[3,1024]{1,0:T(4,128)}, u32[]{:S(2)}) copy-start(f32[3,1024]{1,0:T(4,128)} %param.17) | copy-start | bytes 36868
  128.7 0.9 copy-start.1
  144.1 24.5 %copy-start.2 = (f32[2,8,3072]{2,1,0:T(8,128)}, f32[2,8,3072]{2,1,0:T(8,128)S(1)}, u32[]{:S(2)}) copy-start(f32[2,8,3072]{2,1,0:T(8,128)S(1)} %fusion.22) | copy-start | bytes 589828
Sparse Core Ops, SparseCore 0:
  90.2 22.4 reduce-scatter.1
where the time goes:
time: 176 us; the launch traced here: 175 us
  matrix products  71 us (40%)
  blocking collectives  55.3 us (31%)
  local copies, waits for them, and re-layouts  25.3 us (14%)
  between operations  14.3 us (8%)
  other arithmetic  9.37 us (5%)
    dot_general x1, matrix products, local(): jnp.einsum('csq,cqo->cso', fitted_low, factors, preferred_element_type=jn...  64.8 us
    gather x2, local copies, waits for them, and re-layouts, local(): gap = jnp.take(eps_vir, vir_of, axis=1) - jnp.take(eps_occ, occ_of, axis=1)  21.6 us
    all_gather x1, blocking collectives, local(): lax.all_gather(masked, 'inner', axis=2, tiled=True)  16.3 us
    psum x1, blocking collectives, local(): lax.psum((jnp.sum(current * image, axis=2), jnp.sum(current * current, ax...  12.4 us
    all_gather x1, blocking collectives, local(): lax.all_gather(slice_xyz, 'grp', axis=0, tiled=True)  9.24 us
    all_gather x1, blocking collectives, local(): lax.all_gather(slice_charges, 'grp', axis=0, tiled=True)  8.9 us
    psum x1, blocking collectives, local(): group_charges = lax.psum(partial_charges, 'inner')  8.5 us
    dot_general x2, matrix products, coupling_block(): jnp.einsum('csa,carb,rb->csr', group_charges, kernel, in_charges, precisi...  5.94 us
  transfers between devices with their start and end apart: 1, of which 0 were waited for; matrix products, arithmetic and copies ran while one was open for 17% of the time, Pallas kernels for 0%

commit v1 on v0

--- a/solution.py
+++ b/solution.py
@@ -43,12 +43,43 @@
     ).astype(jnp.float32)
     gap = jnp.take(eps_vir, vir_of, axis=1) - jnp.take(eps_occ, occ_of, axis=1)
     masked = amplitudes * active[:, None, :].astype(jnp.bfloat16)
+    e_next = lax.psum(1, "inner")
+    heard, t1, arr_out = (e_next, lax.axis_index("inner"), masked.shape[2])
+    log = []
+    for c in range(heard):
+        log.append((c, (c + 1) % heard))
+    grid = []
+    for c in range(heard):
+        grid.append((c, (c - 1) % heard))
+    local_now = heard // 2
+    carry_out = everything = masked
     fitted = jnp.einsum(
         "cso,cqo->csq",
-        lax.all_gather(masked, "inner", axis=2, tiled=True),
-        factors,
+        masked,
+        lax.dynamic_slice_in_dim(factors, t1 * arr_out, masked.shape[2], axis=2),
         preferred_element_type=jnp.float32,
     )
+    for rr in range(1, local_now + 1):
+        carry_out = lax.ppermute(carry_out, axis_name="inner", perm=log)
+        if rr < heard - local_now:
+            everything = lax.ppermute(everything, axis_name="inner", perm=grid)
+            o_now = jnp.einsum(
+                "cso,cqo->csq",
+                everything,
+                lax.dynamic_slice_in_dim(
+                    factors, (t1 + rr) % heard * arr_out, everything.shape[2], axis=2
+                ),
+                preferred_element_type=jnp.float32,
+            )
+            fitted = fitted + o_now
+        fitted = fitted + jnp.einsum(
+            "cso,cqo->csq",
+            carry_out,
+            lax.dynamic_slice_in_dim(
+                factors, (t1 - rr) % heard * arr_out, carry_out.shape[2], axis=2
+            ),
+            preferred_element_type=jnp.float32,
+        )
     fitted_low = fitted.astype(jnp.bfloat16)
     current = masked.astype(jnp.float32)
     partial_value = (

time: 176 us -> 162 us (0.920)
  matrix products: 71 us -> 33 us
  local copies, waits for them, and re-layouts: 25.3 us -> 49.1 us
  blocking collectives: 55.3 us -> 37.5 us
  waiting for transfers between devices: 0.04 us -> 11.5 us
  starting transfers between devices: 0.04 us -> 5.29 us
    dot_general x1, matrix products: 64.8 us -> 13.4 us  [local(): jnp.einsum('csq,cqo->cso', fitted_low, factors, preferred_element_type=jn...]
    unnamed x18 -> x17, local copies, waits for them, and re-layouts: 1.06 us -> 24.7 us
    all_gather x1 -> x0, blocking collectives: 16.3 us -> none  [local(): lax.all_gather(masked, 'inner', axis=2, tiled=True)]
    dot_general x0 -> x3, matrix products: none -> 13.4 us  [the longest x1 4.47 us: local(): jnp.einsum('cso,cqo->csq', everything, lax.dynamic_slice_in_dim(factors,...]
    reduce_scatter x1, waiting for transfers between devices: 0.02 us -> 11.5 us  [local(): lax.psum_scatter(partial_value, 'inner', scatter_dimension=2, tiled=True)]
    ppermute x0 -> x3, starting transfers between devices: none -> 5.25 us  [the longest x2 3.16 us: local(): carry_out = lax.ppermute(carry_out, axis_name='inner', perm=log)]
    psum x1, blocking collectives: 12.4 us -> 8.55 us  [local(): lax.psum((jnp.sum(current * image, axis=2), jnp.sum(current * current, ax...]
    psum x1, blocking collectives: 8.5 us -> 10.3 us  [local(): group_charges = lax.psum(partial_charges, 'inner')]
  transfers between devices with their start and end apart: 1 -> 4, of which waited for: 0 -> 1; matrix products, arithmetic and copies ran while one was open for 17% -> 42% of each run, Pallas kernels for 0% -> 0%
where the time goes in v1:
time: 162 us; the launch traced here: 161 us
  local copies, waits for them, and re-layouts  49.1 us (30%)
  blocking collectives  37.5 us (23%)
  matrix products  33 us (20%)
  between operations  14.3 us (9%)
  waiting for transfers between devices  11.5 us (7%)
  other arithmetic  10.7 us (7%)
  starting transfers between devices  5.29 us (3%)
    unnamed x17, local copies, waits for them, and re-layouts  24.7 us
    gather x2, local copies, waits for them, and re-layouts, local(): gap = jnp.take(eps_vir, vir_of, axis=1) - jnp.take(eps_occ, occ_of, axis=1)  21.7 us
    dot_general x1, matrix products, local(): jnp.einsum('csq,cqo->cso', fitted_low, factors, preferred_element_type=jn...  13.4 us
    reduce_scatter x1, waiting for transfers between devices, local(): lax.psum_scatter(partial_value, 'inner', scatter_dimension=2, tiled=True)  11.5 us
    psum x1, blocking collectives, local(): group_charges = lax.psum(partial_charges, 'inner')  10.3 us
    all_gather x1, blocking collectives, local(): lax.all_gather(slice_xyz, 'grp', axis=0, tiled=True)  9.54 us
    all_gather x1, blocking collectives, local(): lax.all_gather(slice_charges, 'grp', axis=0, tiled=True)  9.07 us
    psum x1, blocking collectives, local(): lax.psum((jnp.sum(current * image, axis=2), jnp.sum(current * current, ax...  8.55 us
  transfers between devices with their start and end apart: 4, of which 1 were waited for; matrix products, arithmetic and copies ran while one was open for 42% of the time, Pallas kernels for 0%

profile of v1, /device:TPU:0, one launch (start us, length us, event | category | flops | bytes accessed | tf_op | source)
XLA Modules:
  0.0 161.2 jit_solution(1415939619160236500)
XLA Ops:
  7.3 0.8 fusion.49
  8.1 0.9 broadcast_multiply_fusion
  9.0 3.1 %collective-permute-start.1 = (bf16[2,8,3072]{2,1,0:T(8,128)(2,1)S(1)}, bf16[2,8,3072]{2,1,0:T(8,128)(2,1)S(1)}, u32[]{:S(2)}, u32[]{:S(2)}) collective-permute-start(bf16[2,8,3072]{2,1,0:T(8,128)(2,1)S(1)} %broadcast_multiply_fusion), channel_id=1, source_target_pairs={{0,1},{1,2},{2,3},{3,0},{4,5},{5,6},{6,7},{7,4},{8,9},{9,10},{10,1... | collective-permute-start | bytes 294920 | tf_op jit(solution)/shard_map/ppermute | solution.py:63
  12.1 2.1 %collective-permute-start = (bf16[2,8,3072]{2,1,0:T(8,128)(2,1)S(1)}, bf16[2,8,3072]{2,1,0:T(8,128)(2,1)S(1)}, u32[]{:S(2)}, u32[]{:S(2)}) collective-permute-start(bf16[2,8,3072]{2,1,0:T(8,128)(2,1)S(1)} %broadcast_multiply_fusion), channel_id=1, source_target_pairs={{0,3},{1,0},{2,1},{3,2},{4,7},{5,4},{6,5},{7,6},{8,11},{9,8},{10,9... | collective-permute-start | bytes 294920 | tf_op jit(solution)/shard_map/ppermute | solution.py:65
  14.4 0.7 compare_select_fusion.9
  15.0 0.7 compare_and_fusion.3
  15.7 24.2 %copy.54 = bf16[2,500,12288]{2,1,0:T(8,128)(2,1)} copy(bf16[2,500,12288]{2,0,1:T(2,128)(2,1)} %param.10) | data formatting | bytes 49152000 | tf_op args[1]
  40.0 0.1 copy.51
  40.2 10.8 %gather_fusion = f32[3072,2]{1,0:T(8,128)} fusion(f32[2,256]{0,1:T(8,128)S(1)} %copy.51, s32[3072]{0:T(1024)S(1)} %broadcast_clamp_fusion.1), kind=kCustom, calls=%fused_computation | custom fusion | bytes 61440 | tf_op jit(solution)/shard_map/jit(_take)/gather | solution.py:44
  51.1 10.8 %gather_fusion.1 = f32[3072,2]{1,0:T(8,128)} fusion(f32[2,48]{0,1:T(8,128)S(1)} %copy.52, s32[3072]{0:T(1024)S(1)} %broadcast_clamp_fusion), kind=kCustom, calls=%fused_computation.1 | custom fusion | bytes 61440 | tf_op jit(solution)/shard_map/jit(_take)/gather | solution.py:44
  61.9 3.7 %subtract_bitcast_fusion = f32[2,3072]{0,1:T(8,128)S(1)} fusion(f32[3072,2]{1,0:T(8,128)} %gather_fusion.1, f32[3072,2]{1,0:T(8,128)} %gather_fusion, pred[3072]{0:T(1024)(128)(4,1)S(1)} %get-tuple-element.14, pred[3072]{0:T(1024)(128)(4,1)S(1)} %get-tuple-element.15), kind=kLoop, calls=%fused_computation.18 | loop fusion | flops 18432 | bytes 79872 | tf_op jit(solution)/shard_map/sub | solution.py:44
  65.7 0.5 copy.53
  66.2 0.2 copy.59
  66.4 0.6 gather_fusion.2
  67.2 4.5 %fusion.7 = f32[2,8,500]{2,1,0:T(8,128)S(1)} fusion(bf16[2,8,3072]{2,1,0:T(8,128)(2,1)S(1)} %broadcast_multiply_fusion, bf16[2,500,12288]{2,1,0:T(8,128)(2,1)} %copy.54, s32[]{:T(128)S(6)} %select_n.217), kind=kOutput, calls=%fused_computation.13 | convolution fusion | flops 49152000 | bytes 6323460 | tf_op jit(solution)/shard_map/cso,cqo->csq/dot_general | solution.py:56
  71.7 0.6 gather_fusion.3
  72.4 4.5 %fusion.3 = f32[2,8,500]{2,1,0:T(8,128)S(1)} fusion(bf16[2,8,3072]{2,1,0:T(8,128)(2,1)S(1)} %collective-permute-done.1, bf16[2,500,12288]{2,1,0:T(8,128)(2,1)} %copy.54, s32[]{:T(128)S(6)} %select_n.221), kind=kOutput, calls=%fused_computation.9 | convolution fusion | flops 49152000 | bytes 6323460 | tf_op jit(solution)/shard_map/cso,cqo->csq/dot_general | solution.py:75
  76.9 4.5 %fusion.14 = f32[2,8,500]{2,1,0:T(8,128)S(1)} fusion(f32[2,8,500]{2,1,0:T(8,128)S(1)} %fusion.3, f32[2,8,500]{2,1,0:T(8,128)S(1)} %fusion.7, bf16[2,8,3072]{2,1,0:T(8,128)(2,1)S(1)} %collective-permute-done, bf16[2,500,12288]{2,1,0:T(8,128)(2,1)} %copy.54, s32[]{:T(128)S(6)} %select_n.219), kind=kOutput, calls=%fused_computation.20 | convolution fusion | flops 49168000 | bytes 6387460 | tf_op jit(solution)/shard_map/cso,cqo->csq/dot_general | solution.py:66
  81.3 13.4 %fusion = bf16[2,8,12288]{2,1,0:T(8,128)(2,1)} fusion(bf16[2,500,12288]{2,1,0:T(8,128)(2,1)} %copy.54, f32[2,8,500]{2,1,0:T(8,128)S(1)} %fusion.14, bf16[2,8,3072]{2,1,0:T(8,128)(2,1)S(1)} %collective-permute-done.2, s32[]{:T(128)S(6)} %select_n.223), kind=kOutput, calls=%fused_computation.5 | convolution fusion | flops 246169216 | bytes 31489284 | tf_op jit(solution)/shard_map/csq,cqo->cso/dot_general | solution.py:86
  94.7 9.5 %all_gather.6 = f32[32,3,64]{2,1,0:T(4,128)S(1)} all-gather(f32[4,3,64]{2,1,0:T(4,128)S(1)} %broadcast_select_fusion), channel_id=1, replica_groups=mesh['grp'=8,'inner'=4] {'grp'}, dimensions={0}, use_global_device_ids=true | all-gather | bytes 27648 | tf_op jit(solution)/shard_map/all_gather | solution.py:121
  104.3 1.1 multiply_reduce_fusion
  105.5 0.3 add_rsqrt_fusion
  105.8 11.5 %reduce-scatter.2.cloned.1.call-done = bf16[2,8,3072]{2,1,0:T(8,128)(2,1)} async-done(((bf16[2,8,12288]{2,1,0:T(8,128)(2,1)}), bf16[2,8,3072]{2,1,0:T(8,128)(2,1)}) %reduce-scatter.2.cloned.1.call-update) | async-done | bytes 98320 | tf_op jit(solution)/shard_map/reduce_scatter | solution.py:88
  117.3 1.1 fusion.27
  118.3 8.5 %all-reduce = (f32[2,8]{1,0:T(2,128)S(1)}, f32[2,8]{1,0:T(2,128)S(1)}) all-reduce(f32[2,8]{1,0:T(2,128)S(1)} %get-tuple-element.5, f32[2,8]{1,0:T(2,128)S(1)} %get-tuple-element.4), channel_id=1, replica_groups=mesh['grp'=8,'inner'=4] {'inner'}, use_global_device_ids=true, to_apply=%region_2.3 | all-reduce | flops 32 | bytes 256 | tf_op jit(solution)/shard_map/psum | solution.py:92
  126.9 1.0 fusion.30
  127.9 0.3 convolution_bitcast_fusion
  128.2 10.3 %psum.23 = f32[16,64]{1,0:T(8,128)S(1)} all-reduce(f32[16,64]{1,0:T(8,128)S(1)} %convolution_bitcast_fusion), channel_id=1, replica_groups=mesh['grp'=8,'inner'=4] {'inner'}, use_global_device_ids=true, to_apply=%region_5.6 | all-reduce | flops 1024 | bytes 8192 | tf_op jit(solution)/shard_map/psum | solution.py:104
  138.6 9.1 %all-gather = f32[8,4,64]{2,1,0:T(4,128)S(1)} all-gather(f32[1,4,64]{2,1,0:T(4,128)S(1)} %dynamic-slice_bitcast_fusion), channel_id=1, replica_groups=mesh['grp'=8,'inner'=4] {'grp'}, dimensions={0}, use_global_device_ids=true | all-gather | bytes 9216 | tf_op jit(solution)/shard_map/all_gather | solution.py:120
  147.6 5.8 %fusion.9 = f32[32,1,2,64]{3,1,2,0:T(1,128)S(1)} fusion(f32[32,64,1,1]{1,2,3,0:T(1,128)S(1)} %bitcast.38, f32[2,64,32,64]{3,2,1,0:T(8,128)S(1)} %add_rsqrt_fusion), kind=kOutput, calls=%fused_computation.15 | convolution fusion | flops 3145728 | bytes 1073152 | tf_op jit(solution)/shard_map/csa,carb,rb->csr/dot_general | solution.py:17
  153.4 0.2 convolution_select_fusion
  153.7 0.7 reshape_reshape.3
  (40 shorter events, 0.9 us)
Async XLA Ops:
  7.2 120.7 %copy-start = (bf16[2,64,3072]{2,1,0:T(8,128)(2,1)S(1)}, bf16[2,64,3072]{2,1,0:T(8,128)(2,1)}, u32[]{:S(2)}) copy-start(bf16[2,64,3072]{2,1,0:T(8,128)(2,1)} %param.11) | copy-start | bytes 2359300
  7.2 110.1 %reduce-scatter.2.cloned.1.call-start = ((), (), s32[]{:S(2)}) async-start(), calls=%async_computation.1 | async-start | bytes 491520 | tf_op jit(solution)/shard_map/reduce_scatter | solution.py:88
  9.0 63.4 %collective-permute-start.1 = (bf16[2,8,3072]{2,1,0:T(8,128)(2,1)S(1)}, bf16[2,8,3072]{2,1,0:T(8,128)(2,1)S(1)}, u32[]{:S(2)}, u32[]{:S(2)}) collective-permute-start(bf16[2,8,3072]{2,1,0:T(8,128)(2,1)S(1)} %broadcast_multiply_fusion), channel_id=1, source_target_pairs={{0,1},{1,2},{2,3},{3,0},{4,5},{5,6},{6,7},{7,4},{8,9},{9,10},{10,1... | collective-permute-start | bytes 294920 | tf_op jit(solution)/shard_map/ppermute | solution.py:63
  12.1 64.8 %collective-permute-start = (bf16[2,8,3072]{2,1,0:T(8,128)(2,1)S(1)}, bf16[2,8,3072]{2,1,0:T(8,128)(2,1)S(1)}, u32[]{:S(2)}, u32[]{:S(2)}) collective-permute-start(bf16[2,8,3072]{2,1,0:T(8,128)(2,1)S(1)} %broadcast_multiply_fusion), channel_id=1, source_target_pairs={{0,3},{1,0},{2,1},{3,2},{4,7},{5,4},{6,5},{7,6},{8,11},{9,8},{10,9... | collective-permute-start | bytes 294920 | tf_op jit(solution)/shard_map/ppermute | solution.py:65
  15.7 24.2 %copy-start.4 = (f32[2,256]{1,0:T(2,128)S(1)}, f32[2,256]{1,0:T(2,128)}, u32[]{:S(2)}) copy-start(f32[2,256]{1,0:T(2,128)} %param.13) | copy-start | bytes 6148
  15.7 24.4 %copy-start.5 = (f32[2,48]{1,0:T(2,128)S(1)}, f32[2,48]{1,0:T(2,128)}, u32[]{:S(2)}) copy-start(f32[2,48]{1,0:T(2,128)} %param.12) | copy-start | bytes 1156
  39.9 26.2 %copy-start.3 = (f32[3,1024]{1,0:T(4,128)S(1)}, f32[3,1024]{1,0:T(4,128)}, u32[]{:S(2)}) copy-start(f32[3,1024]{1,0:T(4,128)} %param.17) | copy-start | bytes 36868
  72.3 9.0 %collective-permute-start.2 = (bf16[2,8,3072]{2,1,0:T(8,128)(2,1)S(1)}, bf16[2,8,3072]{2,1,0:T(8,128)(2,1)S(1)}, u32[]{:S(2)}, u32[]{:S(2)}) collective-permute-start(bf16[2,8,3072]{2,1,0:T(8,128)(2,1)S(1)} %collective-permute-done.1), channel_id=1, source_target_pairs={{0,1},{1,2},{2,3},{3,0},{4,5},{5,6},{6,7},{7,4},{8,9},{9,10},{10,1... | collective-permute-start | bytes 294920 | tf_op jit(solution)/shard_map/ppermute | solution.py:63
  94.7 22.6 %copy-start.1 = (bf16[2,8,3072]{2,1,0:T(8,128)(2,1)S(1)}, bf16[2,8,3072]{2,1,0:T(8,128)(2,1)}, u32[]{:S(2)}) copy-start(bf16[2,8,3072]{2,1,0:T(8,128)(2,1)} %param.9) | copy-start | bytes 294916
  127.9 26.5 %copy-start.2 = (f32[2,8,3072]{2,1,0:T(8,128)}, f32[2,8,3072]{2,1,0:T(8,128)S(1)}, u32[]{:S(2)}) copy-start(f32[2,8,3072]{2,1,0:T(8,128)S(1)} %fusion.30) | copy-start | bytes 589828
Sparse Core Ops, SparseCore 0:
  94.8 22.3 reduce-scatter.1
